TPU v7x, 32 devices: a whole 2x2x4 slice. The times are simulated.
32 devices in a mesh: gr: 8 (over z, core), gc: 4 (over y, x).
Axes of the slice: x: 2, y: 2, z: 4, core: 2. Of those that a mesh axis runs over, the one named last changes fastest.
Arguments:
- projectors: bfloat16 [2, 8192, 9216], P(None, ('gr', 'gc')), may hold values from -0.0625 to 0.0625
- wavefunctions: bfloat16 [2, 8192, 512], P(None, ('gr', 'gc')), may hold values from -6 to 6
- coupling: float32 [512, 18, 18], P('gc'), may hold values from -1.5 to 1.5
- atom_order: int32 [512], replicated, may hold values from 0 to 511, each once
Outputs:
- coupled: float32 [9216, 512], P('gc', 'gr')
Inputs may be any that keep to these rules, and one draw needn't show every extreme that they name: `atom_order`: a permutation of the atoms.
All inputs are finite; a program needn't handle non-finite values.
Results may differ from a plain program's by a relative error of at most 0.0003.
Values sent between devices are 32-bit elements; how exact they have to be, the bound alone decides.
A program may use at most 128 MiB of HBM per device.

v0:
```python
import functools
import math

import jax
import jax.numpy as jnp
from jax import lax
from jax.experimental import pallas as pl
from jax.experimental.pallas import tpu as pltpu
from jax.sharding import PartitionSpec as P

MESH = pl.DeviceIdType.MESH
GROUP = 4
LANES = 128
PART = 1152


def plain(projectors, wavefunctions, coupling, atom_order):
    rows_here, nkb = projectors.shape[1:]
    bands = wavefunctions.shape[2]
    atoms = atom_order.shape[0]
    nh = nkb // atoms
    shaped = projectors.reshape(2, rows_here, atoms, nh)
    waves = wavefunctions.reshape(2 * rows_here, bands)
    columns = jnp.take(shaped, atom_order, axis=2).reshape(2 * rows_here, nkb)
    term = lax.dot_general(columns, waves, (((0,), (0,)), ((), ())), preferred_element_type=jnp.float32)
    partial_rows = lax.psum_scatter(2.0 * term, "gc", scatter_dimension=0, tiled=True)
    becp = lax.psum_scatter(partial_rows, "gr", scatter_dimension=1, tiled=True)
    local_atoms = coupling.shape[0]
    becp = becp.reshape(local_atoms, nh, becp.shape[1])
    coupled = jnp.einsum("kij,kjb->kib", coupling, becp, precision=lax.Precision.HIGHEST)
    return coupled.reshape(local_atoms * nh, becp.shape[2])


def path_of(column):
    first, other = ("A", "B") if column % 2 == 0 else ("B", "A")
    order = (first, other, "Z") if (column // 2) % 3 == 1 else (first, "Z", other)
    return order, (1 if column % 2 == 0 else -1)


def divisor(total, most):
    return max(t for t in range(LANES, most + 1, LANES) if total % t == 0)


def kernel(
    size, nh, apo, columns, order_ref, proj_ref, wave_ref, coup_ref, out_ref, fin, mats, nat, strip, acc, oth, rec, strip_sem, send_sem, recv_sem
):
    gr, gc = lax.axis_index("gr"), lax.axis_index("gc")
    core, z = lax.rem(gr, 2), gr // 2
    me = {"A": gc // size["B"], "B": lax.rem(gc, size["B"]), "Z": z}
    half = apo // 2

    slots, _, width = strip.shape
    strips = proj_ref.shape[1] // width

    def load(number):
        slot = number % slots
        return pltpu.make_async_copy(proj_ref.at[:, pl.ds(number * width, width)], strip.at[slot], strip_sem.at[slot])

    for number in range(slots):
        load(number).start()

    def neighbour(dim, way):
        n = size[dim]
        place = lax.rem(me[dim] + n + way, n)
        if dim == "A":
            return {"gr": gr, "gc": place * size["B"] + me["B"]}
        if dim == "B":
            return {"gr": gr, "gc": me["A"] * size["B"] + place}
        return {"gr": place * 2 + core, "gc": gc}

    partner = {"gr": gr + 1 - 2 * core, "gc": gc}
    greeted = [partner]
    for dim in ("A", "B", "Z"):
        if size[dim] > 1:
            greeted.append(neighbour(dim, 1))
        if size[dim] > 2:
            greeted.append(neighbour(dim, -1))
    barrier = pltpu.get_barrier_semaphore()
    for device in greeted:
        pl.semaphore_signal(barrier, inc=1, device_id=device, device_id_type=MESH)

    part = divisor(width, PART)
    for number in range(strips):
        load(number).wait()

        def multiply(t, carry, number=number):
            at = pl.multiple_of(t * part, part)
            term = lax.dot_general(
                strip[number % slots, :, pl.ds(at, part)], wave_ref[...],
                (((0,), (0,)), ((), ())), preferred_element_type=jnp.float32,
            )
            for zz in range(size["Z"]):
                nat[zz, pl.ds(number * width + at, part), :] = term[:, zz * LANES:(zz + 1) * LANES]
            return carry

        lax.fori_loop(0, width // part, multiply, 0)
        if number + slots < strips:
            load(number + slots).start()
    pl.semaphore_wait(barrier, len(greeted))

    def copy(src, dst, column, slot, device):
        return pltpu.make_async_remote_copy(
            src_ref=src, dst_ref=dst, send_sem=send_sem.at[column, slot], recv_sem=recv_sem.at[column, slot],
            device_id=device, device_id_type=MESH,
        )

    def pack(dst, which, column):
        path, _ = path_of(column)

        def body(owner, carry):
            at = {"A": owner // size["B"], "B": lax.rem(owner, size["B"])}
            for i in range(GROUP):
                row = order_ref[owner * apo + which * half + column * GROUP + i] * nh
                for zz in range(size["Z"]):
                    at["Z"] = zz
                    where = tuple(at[d] for d in path)
                    dst[where + (pl.ds(i * nh, nh), slice(None))] = nat[zz, pl.ds(row, nh), :]
            return carry

        lax.fori_loop(0, size["A"] * size["B"], body, 0)

    def add(dst, prefix, src, src_prefix, rest):
        def body(t, carry):
            where = []
            for n in reversed(rest):
                where.insert(0, lax.rem(t, n))
                t = t // n
            where = tuple(where)
            dst[tuple(prefix) + where] = dst[tuple(prefix) + where] + src[tuple(src_prefix) + where]
            return carry

        if rest:
            lax.fori_loop(0, math.prod(rest), body, 0)
        else:
            dst[tuple(prefix)] = dst[tuple(prefix)] + src[tuple(src_prefix)]

    def steps_of(column):
        path, way = path_of(column)
        found = []
        for stage, dim in enumerate(path):
            n = size[dim]
            turn = way if dim == "Z" else 1
            fixed = [me[d] for d in path[:stage]]
            rest = [size[d] for d in path[stage + 1:]]
            for t in range(n - 1):
                sent = lax.rem(me[dim] - turn * (t + 1) + 2 * n, n)
                got = lax.rem(me[dim] - turn * (t + 2) + 2 * n, n)
                found.append((stage, t, fixed + [sent], fixed + [got], rest, neighbour(dim, turn)))
        return found

    started = {}

    def begin(column, slot, made):
        started[column, slot] = made
        made.start()

    def send_step(column, number):
        stage, t, sent, _, _, device = steps[column][number]
        begin(column, number + 1, copy(acc[column].at[tuple(sent)], rec[column][stage + 1].at[t], column, number + 1, device))

    steps = [steps_of(c) for c in range(columns)]
    n_steps = len(steps[0])

    def phase(number, c):
        if number == 0:
            pack(oth[c], 1 - core, c)
            begin(c, 0, copy(oth[c], rec[c][0], c, 0, partner))
            pack(acc[c], core, c)
            return
        started[c, number - 1].wait_recv()
        if number == 1:
            path, _ = path_of(c)
            add(acc[c], (), rec[c][0], (), [size[d] for d in path])
        else:
            stage, t, _, got, rest, _ = steps[c][number - 2]
            add(acc[c], got, rec[c][stage + 1], [t], rest)
        if number <= n_steps:
            send_step(c, number - 1)
            return
        path, _ = path_of(c)
        mine = tuple(me[d] for d in path)
        at = pl.ds(c * GROUP * nh, GROUP * nh)
        for i in range(GROUP):
            becp = 2.0 * acc[c][mine + (pl.ds(i * nh, nh), slice(None))]
            fin[core, pl.ds((c * GROUP + i) * nh, nh), :] = jnp.dot(
                mats[:, pl.ds(core * half + c * GROUP + i, 1), :].reshape(nh, nh), becp,
                precision=lax.Precision.HIGHEST, preferred_element_type=jnp.float32,
            )
        begin(c, n_steps + 1, copy(fin.at[core, at], fin.at[core, at], c, n_steps + 1, partner))

    lag = [0, 1] + [3 * i + 1 for i in range(1, n_steps + 1)]
    for tick in range(columns + lag[-1]):
        if tick == lag[2]:
            for i in range(nh):
                mats[i] = coup_ref[i].T
        for number in reversed(range(n_steps + 2)):
            c = tick - lag[number]
            if 0 <= c < columns:
                phase(number, c)

    def turn(which):
        rows = fin.shape[1]

        def body(t, carry):
            block = fin[which, pl.ds(pl.multiple_of(t * LANES, LANES), LANES), :].T
            own = LANES // 2
            at = pl.multiple_of(which * rows + t * LANES, LANES)
            out_ref[:, pl.ds(at, LANES)] = jnp.where(core == 0, block[:own], block[own:])
            return carry

        lax.fori_loop(0, rows // LANES, body, 0)

    turn(core)
    for c in range(columns):
        started[c, n_steps + 1].wait_recv()
    turn(1 - core)
    for c in range(columns):
        for slot in range(n_steps + 2):
            started[c, slot].wait_send()


def routed(size, projectors, wavefunctions, coupling, atom_order):
    rows_here, nkb = projectors.shape[1:]
    bands = wavefunctions.shape[2]
    atoms = atom_order.shape[0]
    nh, apo = nkb // atoms, coupling.shape[0]
    columns = apo // 2 // GROUP
    n_steps = sum(size.values()) - 3
    tile = (GROUP * nh, LANES)
    width = divisor(nkb, 1152)
    acc, rec = [], []
    for c in range(columns):
        n1, n2, n3 = (size[d] for d in path_of(c)[0])
        acc.append(pltpu.VMEM((n1, n2, n3) + tile, jnp.float32))
        rec.append([
            pltpu.VMEM((n1, n2, n3) + tile, jnp.float32),
            pltpu.VMEM((n1 - 1, n2, n3) + tile, jnp.float32),
            pltpu.VMEM((n2 - 1, n3) + tile, jnp.float32),
            pltpu.VMEM((n3 - 1,) + tile, jnp.float32),
        ])
    out = pl.pallas_call(
        functools.partial(kernel, size, nh, apo, columns),
        out_shape=jax.ShapeDtypeStruct((LANES // 2, apo * nh), jnp.float32),
        in_specs=[
            pl.BlockSpec(memory_space=pltpu.SMEM),
            pl.BlockSpec(memory_space=pl.ANY),
            pl.BlockSpec(memory_space=pltpu.VMEM),
            pl.BlockSpec(memory_space=pltpu.VMEM),
        ],
        out_specs=pl.BlockSpec(memory_space=pltpu.VMEM),
        scratch_shapes=[
            pltpu.VMEM((2, apo * nh // 2, LANES), jnp.float32),
            pltpu.VMEM((nh, apo, nh), jnp.float32),
            pltpu.VMEM((size["Z"], nkb, LANES), jnp.float32),
            pltpu.VMEM((3, 2 * rows_here, width), projectors.dtype),
            acc,
            list(acc),
            rec,
            pltpu.SemaphoreType.DMA((3,)),
            pltpu.SemaphoreType.DMA((columns, n_steps + 2)),
            pltpu.SemaphoreType.DMA((columns, n_steps + 2)),
        ],
        compiler_params=pltpu.CompilerParams(
            collective_id=0, has_side_effects=True, vmem_limit_bytes=67_043_328
        ),
    )(
        atom_order, projectors.reshape(2 * rows_here, nkb), wavefunctions.reshape(2 * rows_here, bands),
        jnp.transpose(coupling, (1, 2, 0)),
    )
    return out.T


def solution(mesh):
    gr, gc = mesh.shape["gr"], mesh.shape["gc"]
    wide = max(d for d in range(1, math.isqrt(gc) + 1) if gc % d == 0)
    size = {"A": wide, "B": gc // wide, "Z": gr // 2}

    def shards(projectors, wavefunctions, coupling, atom_order):
        fits = (
            gr % 2 == 0
            and min(size.values()) > 1
            and wavefunctions.shape[2] == size["Z"] * LANES
            and coupling.shape[0] % (2 * GROUP) == 0
            and projectors.shape[2] % (2 * gc * LANES) == 0
        )
        if fits:
            return routed(size, projectors, wavefunctions, coupling, atom_order)
        return plain(projectors, wavefunctions, coupling, atom_order)

    return jax.shard_map(
        shards,
        mesh=mesh,
        in_specs=(
            P(None, ("gr", "gc"), None),
            P(None, ("gr", "gc"), None),
            P("gc", None, None),
            P(),
        ),
        out_specs=P("gc", "gr"),
        check_vma=False,
    )
```

profile of v0, /device:TPU:0, one launch (start us, length us, event | category | flops | bytes accessed | tf_op | source)
XLA Modules:
  0.0 105.4 jit_solution(7595387038678311632)
XLA Ops:
  0.0 103.4 %shard_map.46 = f32[64,2304]{1,0:T(8,128)} custom-call(s32[512]{0:T(512)} %order_ref.1, bf16[512,9216]{1,0:T(8,128)(2,1)} %bitcast.4, bf16[512,512]{1,0:T(8,128)(2,1)} %bitcast.6, f32[18,18,128]{2,1,0:T(8,128)} %bitcast.7), custom_call_target="tpu_custom_call" | custom-call | tf_op jit(solution)/shard_map/pallas_call | solution.py:241
  103.4 1.9 %copy.6 = f32[2304,64]{0,1:T(8,128)} copy(f32[2304,64]{0,1:T(8,128)} %bitcast.5) | data formatting | bytes 1179648
where the time goes:
time: 106 us; the launch traced here: 105 us
  Pallas kernels  103 us (97%)
  local copies, waits for them, and re-layouts  1.92 us (2%)
    pallas_call x1, Pallas kernels, routed(): pl.pallas_call(functools.partial(kernel, size, nh, apo, columns), out_sha...  103 us

commit v1 on v0

v1 whole, which is shorter than its diff:
```python
import functools
import math

import jax
import jax.numpy as jnp
from jax import lax
from jax.experimental import pallas as pl
from jax.experimental.pallas import tpu as pltpu
from jax.sharding import PartitionSpec as P

MESH = pl.DeviceIdType.MESH
GROUP = 8
GROUPS = 8
LANES = 128
STRIP = 1152
BATCHES = ((0, 1, 2, 3), (4, 5, 6, 7), (0, 1, 2, 3), (4, 5, 6, 7))
FIRST_PASS = 2
PACKS = 4
RESULTS = 4
MULTIPLY, COUPLINGS = -1, -2

UNITS = (
    (0, 0, "ABZ"), (1, 0, "ZBA"), (2, 0, "BAZ"), (3, 0, "ZAB"),
    (4, 0, "ABZ"), (5, 0, "ZAB"), (6, 0, "ZBA"), (7, 0, "ZBA"),
    (0, 1, "BAZ"), (1, 1, "ABZ"), (2, 1, "BAZ"), (3, 1, "ABZ"),
    (4, 1, "BAZ"), (5, 1, "ABZ"), (6, 1, "BAZ"), (7, 1, "ABZ"),
)
SPLIT = (0, 1, 2)
ORDER = (
    -1, -1, 0, 1, 2, 128, 7, 129, 130, 16, 17, 18, 3, -1, -1, 11, 8, 6, 27, 19, 112, 4, 13, 10, 24, 32, 15, 113, -2,
    33, 29, 114, 22, 23, 43, 12, 31, 26, 35, 9, 45, 49, 20, 5, 38, 21, 14, 40, 47, 30, 48, 51, 39, 37, 61, 54, 59,
    25, 63, 75, 56, 42, 28, 36, 77, 64, 55, 46, 53, 41, 58, 34, 72, 74, 44, 67, 80, 62, 70, 71, 79, 78, 52, 50, 95,
    57, 69, 93, 86, 68, 65, 91, 90, 96, 60, 66, 83, 87, 85, 73, 84, 107, 111, 109, 88, 81, 100, 82, 102, 106, 99,
    76, 103, 94, 98, 101, 89, 92, 110, 108, 104, 105, 97,
)


def receiving():
    found, count = {}, 0
    for u, (_, h, path) in enumerate(UNITS):
        at_z = path.index("Z")
        if at_z == 0:
            sets = [(0,), (3, 6), (4, 1), (2,)]
        elif at_z == 1:
            sets = [(0,), (1,), (3, 6), (4, 2)]
        else:
            sets = [(0,), (1,), (2,), (3, 6), (4,)] + ([(5,)] if h == 1 else [])
        if u in SPLIT:
            sets.append((7,))
        for slots in sets:
            found.update({(u, slot): count for slot in slots})
            count += 1
    return found, count


RECEIVING, RECEIVES = receiving()


def plain(projectors, wavefunctions, coupling, atom_order):
    rows_here, nkb = projectors.shape[1:]
    bands = wavefunctions.shape[2]
    atoms = atom_order.shape[0]
    nh = nkb // atoms
    shaped = projectors.reshape(2, rows_here, atoms, nh)
    waves = wavefunctions.reshape(2 * rows_here, bands)
    columns = jnp.take(shaped, atom_order, axis=2).reshape(2 * rows_here, nkb)
    term = lax.dot_general(columns, waves, (((0,), (0,)), ((), ())), preferred_element_type=jnp.float32)
    partial_rows = lax.psum_scatter(2.0 * term, "gc", scatter_dimension=0, tiled=True)
    becp = lax.psum_scatter(partial_rows, "gr", scatter_dimension=1, tiled=True)
    local_atoms = coupling.shape[0]
    becp = becp.reshape(local_atoms, nh, becp.shape[1])
    coupled = jnp.einsum("kij,kjb->kib", coupling, becp, precision=lax.Precision.HIGHEST)
    return coupled.reshape(local_atoms * nh, becp.shape[2])


def kernel(
    size, nh, apo, order_in, proj_ref, wave_in, coup_in, out_ref, order_ref, turned, fin, mats, nat, strip, wave, coup,
    oth, rec, strip_sem, load_sem, send_sem, recv_sem, fin_send, fin_recv, out_sem,
):
    gr, gc = lax.axis_index("gr"), lax.axis_index("gc")
    core, z = lax.rem(gr, 2), gr // 2
    me = {"A": gc // size["B"], "B": lax.rem(gc, size["B"])}
    half = apo // 2
    rows = GROUP * nh
    side = z // 2
    near, far = side, 1 - side
    way = 1 - 2 * side
    end = (z == 0) | (z == size["Z"] - 1)
    middle = jnp.logical_not(end)

    def at(a, b, zz):
        return {"gr": zz * 2 + core, "gc": a * size["B"] + b}

    partner = {"gr": gr + 1 - 2 * core, "gc": gc}
    other = {"A": at(1 - me["A"], me["B"], z), "B": at(me["A"], 1 - me["B"], z)}
    inward = at(me["A"], me["B"], z + way)
    outward = at(me["A"], me["B"], lax.rem(z - way + size["Z"], size["Z"]))

    strips = proj_ref.shape[1] // STRIP

    def load(number):
        return pltpu.make_async_copy(proj_ref.at[:, pl.ds(number * STRIP, STRIP)], strip.at[number], strip_sem.at[number])

    wave_loads = [
        pltpu.make_async_copy(wave_in.at[:, pl.ds(zz * LANES, LANES)], wave.at[:, pl.ds(i * LANES, LANES)], load_sem.at[i])
        for i, zz in enumerate((0, 3, 1, 2))
    ]
    coup_load = pltpu.make_async_copy(coup_in, coup, load_sem.at[4])
    order_load = pltpu.make_async_copy(order_in, order_ref, load_sem.at[5])
    wave_loads[0].start()
    wave_loads[1].start()
    for number in range(strips):
        load(number).start()
    order_load.start()
    wave_loads[2].start()
    wave_loads[3].start()
    coup_load.start()

    greeted = [partner, other["A"], other["B"], inward, outward]
    barrier = pltpu.get_barrier_semaphore()
    for device in greeted:
        pl.semaphore_signal(barrier, inc=1, device_id=device, device_id_type=MESH)

    def multiply(batch):
        h = int(batch >= FIRST_PASS)
        if batch in (0, FIRST_PASS):
            wave_loads[2 * h].wait()
            wave_loads[2 * h + 1].wait()
        if h == 0:
            for number in BATCHES[batch]:
                load(number).wait()
        for number in BATCHES[batch]:
            term = lax.dot_general(
                strip[number], wave[:, 2 * h * LANES:2 * (h + 1) * LANES],
                (((0,), (0,)), ((), ())), preferred_element_type=jnp.float32,
            )
            for i in range(2):
                nat[2 * h + i, pl.ds(number * STRIP, STRIP), :] = term[:, i * LANES:(i + 1) * LANES]

    def first_of(u):
        path = UNITS[u][2]
        return far if path[0] == "Z" else 1 - me[path[0]]

    def gather(u, which, store, fixed=None):
        g, h, path = UNITS[u]

        def body(t, carry):
            of = {}
            if fixed is None or path[0] == "Z":
                of = {"A": t // size["B"], "B": lax.rem(t, size["B"])}
            else:
                of = {path[0]: fixed, "B" if path[0] == "A" else "A": t}
            owner = of["A"] * size["B"] + of["B"]
            for i in range(GROUP):
                row = order_ref[owner * apo + which * half + g * GROUP + i] * nh
                for zi in ((0, 1) if fixed is None or path[0] != "Z" else (fixed,)):
                    of["Z"] = zi
                    where = tuple(of[d] for d in path) + (pl.ds(i * nh, nh), slice(None))
                    store(where, nat[2 * h + zi, pl.ds(row, nh), :])
            return carry

        lax.fori_loop(0, size["A"] * size["B"] if fixed is None or path[0] == "Z" else 2, body, 0)

    def add(dst, prefix, src):
        rest = src.shape[:-2]
        if len(rest) == 2:
            def body(t, carry):
                where = (t // rest[1], lax.rem(t, rest[1]))
                dst[tuple(prefix) + where] = dst[tuple(prefix) + where] + src[where]
                return carry

            lax.fori_loop(0, math.prod(rest), body, 0)
        elif rest:
            for t in range(rest[0]):
                dst[tuple(prefix) + (t,)] = dst[tuple(prefix) + (t,)] + src[t]
        else:
            dst[tuple(prefix)] = dst[tuple(prefix)] + src[...]

    def copy(u, slot, src, dst, device):
        return pltpu.make_async_remote_copy(
            src_ref=src, dst_ref=dst, send_sem=send_sem.at[sending(u, slot)], recv_sem=recv_sem.at[RECEIVING[u, slot]],
            device_id=device, device_id_type=MESH,
        )

    def sending(u, slot):
        if slot == 0:
            return len(UNITS) + packs.index(u) % PACKS
        if slot == 7:
            return len(UNITS) + PACKS + SPLIT.index(u)
        if slot == 5:
            return len(UNITS) + PACKS + len(SPLIT) + UNITS[u][0]
        return u

    def packed(u):
        return oth.at[packs.index(u) % PACKS]

    def head(u, rest):
        if u not in SPLIT:
            return ()
        return (1 - first_of(u) if rest else first_of(u),)

    def buffers(u, slot):
        if slot in (0, 7):
            return rec[u][0].at[head(u, slot == 7)] if u in SPLIT else rec[u][0]
        return rec[u][slot]

    def send(u, slot):
        g, h, path = UNITS[u]
        d1, d2 = [d for d in path if d != "Z"]
        me1, me2 = me[d1], me[d2]
        to = buffers(u, slot)
        if slot in (0, 7):
            return copy(u, slot, packed(u).at[head(u, slot == 7)] if u in SPLIT else packed(u), to, partner)
        at_z = path.index("Z")
        place = (me1, me2)[:at_z]
        src = {3: place + (far,), 4: place + (far,), 5: place + (near,), 6: place + (near,)}
        if at_z == 0:
            src[1], src[2] = (near, 1 - me1), (near, me1, 1 - me2)
        elif at_z == 1:
            src[1], src[2] = (1 - me1,), (me1, near, 1 - me2)
        else:
            src[1], src[2] = (1 - me1,), (me1, 1 - me2)
        device = {1: other[d1], 2: other[d2], 3: inward, 4: inward, 5: inward, 6: outward}[slot]
        return copy(u, slot, rec[u][0].at[src[slot]], to, device)

    def arrived(u, slot):
        to = buffers(u, slot)
        copy(u, slot, to, to, partner).wait_recv()

    def fin_copy(g, turn):
        part = fin.at[core, pl.ds(g * rows, rows)]
        return pltpu.make_async_remote_copy(
            src_ref=part, dst_ref=part, send_sem=fin_send.at[turn % 2], recv_sem=fin_recv.at[g],
            device_id=partner, device_id_type=MESH,
        )

    def ready(groups):
        return {t for t in range(blocks) if all(g in groups for g in range(t * LANES // rows, (t * LANES + LANES - 1) // rows + 1))}

    def result(t, mine, turn):
        which = core if mine else 1 - core
        columns = pl.ds(pl.multiple_of((which * blocks + t) * LANES, LANES), LANES)
        return pltpu.make_async_copy(turned.at[:, columns], out_ref.at[:, columns], out_sem.at[turn % RESULTS])

    def turn(t, mine):
        which = core if mine else 1 - core
        block = fin[which, pl.ds(t * LANES, LANES), :].T
        own = LANES // 2
        to = pl.ds(pl.multiple_of((which * blocks + t) * LANES, LANES), LANES)
        turned[:, to] = jnp.where(core == 0, block[:own], block[own:])

    def come(g):
        part = fin.at[1 - core, pl.ds(g * rows, rows)]
        pltpu.make_async_remote_copy(
            src_ref=part, dst_ref=part, send_sem=fin_send.at[0], recv_sem=fin_recv.at[g],
            device_id=partner, device_id_type=MESH,
        ).wait_recv()

    def fetch(role, groups):
        came = state[role][1]
        for g in groups:
            if g not in came:
                come(g)
                came.append(g)

    def turns(role):
        made, came, mine, theirs = state[role]
        found = [(t, True) for t in sorted(ready(made) - mine)] + [(t, False) for t in sorted(ready(came) - theirs)]
        for t, own in found:
            turn(t, own)
            (mine if own else theirs).add(t)
        return found

    def put(role, found):
        given = results[role]
        for t, own in found:
            if len(given) >= RESULTS:
                result(*given[-RESULTS], len(given) - RESULTS).wait()
            result(t, own, len(given)).start()
            given.append((t, own))

    def final(u, own, others, role):
        g = UNITS[u][0]
        made = state[role][0]
        fetch(role, made[:-1])
        found = turns(role)
        for i in range(GROUP):
            here = (pl.ds(i * nh, nh), slice(None))
            becp = rec[u][0][own + here]
            for slot in others:
                becp = becp + rec[u][slot][here]
            fin[core, pl.ds((g * GROUP + i) * nh, nh), :] = jnp.dot(
                mats[:, pl.ds(core * half + g * GROUP + i, 1), :].reshape(nh, nh), 2.0 * becp,
                precision=lax.Precision.HIGHEST, preferred_element_type=jnp.float32,
            )
        if len(made) >= 2:
            fin_copy(made[-2], len(made) - 2).wait_send()
        fin_copy(g, len(made)).start()
        made.append(g)
        put(role, found)
        if len(made) == GROUPS:
            put(role, turns(role))
            fetch(role, made)
            put(role, turns(role))

    blocks = GROUPS * rows // LANES
    state = {role: ([], [], set(), set()) for role in ("end", "middle")}
    results = {"end": [], "middle": []}
    packs = [code % 16 for code in ORDER if 0 <= code < 16]
    pending = {"end": {}, "middle": {}}

    def start(u, slot, role):
        roles = ("end", "middle") if role == "all" else (role,)
        key = sending(u, slot)
        before = {pending[r].get(key) for r in roles}
        assert len(before) == 1
        for old in before:
            if old is not None:
                send(*old).wait_send()
        send(u, slot).start()
        for r in roles:
            pending[r][key] = (u, slot)

    def finish(role):
        for u, slot in pending[role].values():
            send(u, slot).wait_send()
        made, given = state[role][0], results[role]
        for turn in range(len(made) - 2, len(made)):
            fin_copy(made[turn], turn).wait_send()
        for turn in range(len(given) - RESULTS, len(given)):
            result(*given[turn], turn).wait()

    def relay(u, slot, place, out):
        @pl.when(middle)
        def _():
            arrived(u, slot)
            add(rec[u][0], place, rec[u][slot])
            start(u, out, "middle")

    def phase(p, u):
        g, h, path = UNITS[u]
        d1, d2 = [d for d in path if d != "Z"]
        me1, me2 = me[d1], me[d2]
        at_z = path.index("Z")
        if p in (0, 8):
            place = packs.index(u)
            target = packed(u)

            def keep(where, value):
                target[where] = value

            if p == 0 and place >= PACKS:
                before = packs[place - PACKS]
                for slot in (0, 7) if before in SPLIT else (0,):
                    send(before, slot).wait_send()
                    for r in ("end", "middle"):
                        del pending[r][sending(before, slot)]
            gather(u, 1 - core, keep, *head(u, p == 8))
            start(u, 7 if p == 8 else 0, "all")
            return
        if p in (1, 7):
            arrived(u, 0 if p == 1 else 7)
            both = rec[u][0]

            def total(where, value):
                both[where] = both[where] + value

            gather(u, core, total, *head(u, p == 7))
            if p == 7:
                return
        if at_z == 2:
            if p == 1:
                start(u, 1, "all")
            elif p == 2:
                arrived(u, 1)
                add(rec[u][0], (me1,), rec[u][1])
                start(u, 2, "all")
            elif p == 3:
                arrived(u, 2)
                add(rec[u][0], (me1, me2), rec[u][2])

                @pl.when(end)
                def _():
                    start(u, 3, "end")
                    if h == 1:
                        start(u, 5, "end")
            elif p == 4:
                relay(u, 3, (me1, me2, far), 4)
            elif p == 5 and h == 0:
                relay(u, 4, (me1, me2, near), 6)
            elif p == 5:
                @pl.when(middle)
                def _():
                    arrived(u, 5)
                    arrived(u, 4)
                    final(u, (me1, me2, near), (5, 4), "middle")
            elif h == 0:
                @pl.when(end)
                def _():
                    arrived(u, 6)
                    final(u, (me1, me2, near), (6,), "end")
        elif at_z == 1:
            if p == 1:
                start(u, 1, "all")
            elif p == 2:
                arrived(u, 1)
                add(rec[u][0], (me1,), rec[u][1])

                @pl.when(end)
                def _():
                    start(u, 3, "end")
            elif p == 3:
                relay(u, 3, (me1, far), 4)
            elif p == 4:
                relay(u, 4, (me1, near), 6)
            elif p == 5:
                @pl.when(end)
                def _():
                    arrived(u, 6)
                    add(rec[u][0], (me1, near), rec[u][6])
                    start(u, 2, "end")
            else:
                @pl.when(end)
                def _():
                    arrived(u, 2)
                    final(u, (me1, near, me2), (2,), "end")
        else:
            if p == 1:
                @pl.when(end)
                def _():
                    start(u, 3, "end")
            elif p == 2:
                relay(u, 3, (far,), 4)
            elif p == 3:
                relay(u, 4, (near,), 6)
            elif p == 4:
                @pl.when(end)
                def _():
                    arrived(u, 6)
                    add(rec[u][0], (near,), rec[u][6])
                    start(u, 1, "end")
            elif p == 5:
                @pl.when(end)
                def _():
                    arrived(u, 1)
                    add(rec[u][0], (near, me1), rec[u][1])
                    start(u, 2, "end")
            else:
                @pl.when(end)
                def _():
                    arrived(u, 2)
                    final(u, (near, me1, me2), (2,), "end")

    multiplied, greeting = 0, True
    for code in ORDER:
        if code == MULTIPLY:
            multiply(multiplied)
            multiplied += 1
        elif code == COUPLINGS:
            coup_load.wait()
            for i in range(nh):
                mats[i] = coup[i].T
        else:
            if greeting:
                pl.semaphore_wait(barrier, len(greeted))
                order_load.wait()
                greeting = False
            phase(code // 16, code % 16)

    @pl.when(end)
    def _():
        finish("end")

    @pl.when(middle)
    def _():
        finish("middle")


def routed(size, projectors, wavefunctions, coupling, atom_order):
    rows_here, nkb = projectors.shape[1:]
    bands = wavefunctions.shape[2]
    atoms = atom_order.shape[0]
    nh, apo = nkb // atoms, coupling.shape[0]
    tile = (GROUP * nh, LANES)
    f32 = jnp.float32
    rec = []
    for _, h, path in UNITS:
        if path[0] == "Z":
            shapes = {0: (2, 2, 2), 1: (2,), 2: (), 3: (2, 2), 4: (2, 2), 6: (2, 2)}
        elif path[1] == "Z":
            shapes = {0: (2, 2, 2), 1: (2, 2), 2: (), 3: (2,), 4: (2,), 6: (2,)}
        else:
            shapes = {0: (2, 2, 2), 1: (2, 2), 2: (2,), 3: (), 4: ()}
            shapes[6 if h == 0 else 5] = ()
        rec.append({slot: pltpu.VMEM(shape + tile, f32) for slot, shape in shapes.items()})
    out = pl.pallas_call(
        functools.partial(kernel, size, nh, apo),
        out_shape=jax.ShapeDtypeStruct((LANES // 2, apo * nh), f32),
        in_specs=[
            pl.BlockSpec(memory_space=pl.ANY),
            pl.BlockSpec(memory_space=pl.ANY),
            pl.BlockSpec(memory_space=pl.ANY),
            pl.BlockSpec(memory_space=pl.ANY),
        ],
        out_specs=pl.BlockSpec(memory_space=pl.ANY),
        scratch_shapes=[
            pltpu.SMEM((atoms,), jnp.int32),
            pltpu.VMEM((LANES // 2, apo * nh), f32),
            pltpu.VMEM((2, apo * nh // 2, LANES), f32),
            pltpu.VMEM((nh, apo, nh), f32),
            pltpu.VMEM((size["Z"], nkb, LANES), f32),
            pltpu.VMEM((nkb // STRIP, 2 * rows_here, STRIP), projectors.dtype),
            pltpu.VMEM((2 * rows_here, bands), wavefunctions.dtype),
            pltpu.VMEM((nh, nh, apo), f32),
            pltpu.VMEM((PACKS, 2, 2, 2) + tile, f32),
            rec,
            pltpu.SemaphoreType.DMA((nkb // STRIP,)),
            pltpu.SemaphoreType.DMA((6,)),
            pltpu.SemaphoreType.DMA((len(UNITS) + PACKS + len(SPLIT) + GROUPS,)),
            pltpu.SemaphoreType.DMA((RECEIVES,)),
            pltpu.SemaphoreType.DMA((2,)),
            pltpu.SemaphoreType.DMA((GROUPS,)),
            pltpu.SemaphoreType.DMA((RESULTS,)),
        ],
        compiler_params=pltpu.CompilerParams(
            collective_id=0, has_side_effects=True, vmem_limit_bytes=67_043_328
        ),
    )(
        atom_order, projectors.reshape(2 * rows_here, nkb), wavefunctions.reshape(2 * rows_here, bands),
        jnp.transpose(coupling, (1, 2, 0)),
    )
    return out.T


def solution(mesh):
    gr, gc = mesh.shape["gr"], mesh.shape["gc"]
    wide = max(d for d in range(1, math.isqrt(gc) + 1) if gc % d == 0)
    size = {"A": wide, "B": gc // wide, "Z": gr // 2}

    def shards(projectors, wavefunctions, coupling, atom_order):
        fits = (
            gr % 2 == 0
            and size == {"A": 2, "B": 2, "Z": 4}
            and wavefunctions.shape[2] == size["Z"] * LANES
            and coupling.shape[0] == 2 * GROUP * GROUPS
            and coupling.shape[0] == LANES
            and projectors.shape[2] == sum(len(b) for b in BATCHES) // 2 * STRIP
        )
        if fits:
            return routed(size, projectors, wavefunctions, coupling, atom_order)
        return plain(projectors, wavefunctions, coupling, atom_order)

    return jax.shard_map(
        shards,
        mesh=mesh,
        in_specs=(
            P(None, ("gr", "gc"), None),
            P(None, ("gr", "gc"), None),
            P("gc", None, None),
            P(),
        ),
        out_specs=P("gc", "gr"),
        check_vma=False,
    )
```

time: 106 us -> 84.1 us (0.79)
  Pallas kernels: 103 us -> 82 us
    pallas_call x1, Pallas kernels: 103 us -> 82 us  [routed(): pl.pallas_call(functools.partial(kernel, size, nh, apo), out_shape=jax.Sh...]
where the time goes in v1:
time: 84.1 us; the launch traced here: 84 us
  Pallas kernels  82 us (98%)
  local copies, waits for them, and re-layouts  1.92 us (2%)
    pallas_call x1, Pallas kernels, routed(): pl.pallas_call(functools.partial(kernel, size, nh, apo), out_shape=jax.Sh...  82 us
    unnamed x1, local copies, waits for them, and re-layouts  1.92 us

profile of v1, /device:TPU:0, one launch (start us, length us, event | category | flops | bytes accessed | tf_op | source)
XLA Modules:
  0.0 84.0 jit_solution(14053747372066734389)
XLA Ops:
  0.0 82.0 %shard_map.46 = f32[64,2304]{1,0:T(8,128)} custom-call(s32[512]{0:T(512)} %order_in.1, bf16[512,9216]{1,0:T(8,128)(2,1)} %bitcast.4, bf16[512,512]{1,0:T(8,128)(2,1)} %bitcast.6, f32[18,18,128]{2,1,0:T(8,128)} %bitcast.7), custom_call_target="tpu_custom_call" | custom-call | tf_op jit(solution)/shard_map/pallas_call | solution.py:496
  82.1 1.9 %copy.6 = f32[2304,64]{0,1:T(8,128)} copy(f32[2304,64]{0,1:T(8,128)} %bitcast.5) | data formatting | bytes 1179648

commit v2 on v1

--- a/solution.py
+++ b/solution.py
@@ -13,25 +13,25 @@
 GROUPS = 8
 LANES = 128
 STRIP = 1152
-BATCHES = ((0, 1, 2, 3), (4, 5, 6, 7), (0, 1, 2, 3), (4, 5, 6, 7))
-FIRST_PASS = 2
+BATCHES = ((0, 1), (2, 3), (4, 5), (6, 7), (0, 1, 2, 3), (4, 5, 6, 7))
+FIRST_PASS = 4
 PACKS = 4
 RESULTS = 4
 MULTIPLY, COUPLINGS = -1, -2
 
 UNITS = (
-    (0, 0, "ABZ"), (1, 0, "ZBA"), (2, 0, "BAZ"), (3, 0, "ZAB"),
+    (0, 0, "ZAB"), (1, 0, "ABZ"), (2, 0, "BAZ"), (3, 0, "ZBA"),
     (4, 0, "ABZ"), (5, 0, "ZAB"), (6, 0, "ZBA"), (7, 0, "ZBA"),
     (0, 1, "BAZ"), (1, 1, "ABZ"), (2, 1, "BAZ"), (3, 1, "ABZ"),
     (4, 1, "BAZ"), (5, 1, "ABZ"), (6, 1, "BAZ"), (7, 1, "ABZ"),
 )
 SPLIT = (0, 1, 2)
 ORDER = (
-    -1, -1, 0, 1, 2, 128, 7, 129, 130, 16, 17, 18, 3, -1, -1, 11, 8, 6, 27, 19, 112, 4, 13, 10, 24, 32, 15, 113, -2,
-    33, 29, 114, 22, 23, 43, 12, 31, 26, 35, 9, 45, 49, 20, 5, 38, 21, 14, 40, 47, 30, 48, 51, 39, 37, 61, 54, 59,
-    25, 63, 75, 56, 42, 28, 36, 77, 64, 55, 46, 53, 41, 58, 34, 72, 74, 44, 67, 80, 62, 70, 71, 79, 78, 52, 50, 95,
-    57, 69, 93, 86, 68, 65, 91, 90, 96, 60, 66, 83, 87, 85, 73, 84, 107, 111, 109, 88, 81, 100, 82, 102, 106, 99,
-    76, 103, 94, 98, 101, 89, 92, 110, 108, 104, 105, 97,
+    -1, -1, -1, -1, 1, 2, 7, 130, 129, 17, 18, 23, -1, 4, -1, 10, 0, 20, 114, 26, 11, 128, 16, 27, 113, 39, 15, 31,
+    112, 3, -2, 32, 19, 14, 33, 42, 6, 36, 55, 30, 22, 13, 29, 12, 35, 28, 52, 48, 38, 51, 47, 34, 43, 68, 49, 5,
+    21, 54, 58, 44, 9, 37, 25, 45, 8, 24, 63, 74, 46, 84, 50, 53, 66, 60, 71, 64, 79, 59, 65, 75, 41, 95, 40, 67,
+    61, 70, 62, 77, 76, 81, 57, 69, 78, 87, 90, 56, 100, 93, 82, 106, 83, 73, 97, 80, 85, 86, 103, 94, 72, 96, 89,
+    92, 111, 110, 105, 99, 98, 101, 102, 91, 88, 107, 108, 109, 104,
 )
 
 

time: 84.1 us -> 81.5 us (0.969)
  Pallas kernels: 82 us -> 79.4 us
    pallas_call x1, Pallas kernels: 82 us -> 79.4 us  [routed(): pl.pallas_call(functools.partial(kernel, size, nh, apo), out_shape=jax.Sh...]
where the time goes in v2:
time: 81.5 us; the launch traced here: 81.4 us
  Pallas kernels  79.4 us (97%)
  local copies, waits for them, and re-layouts  1.92 us (2%)
    pallas_call x1, Pallas kernels, routed(): pl.pallas_call(functools.partial(kernel, size, nh, apo), out_shape=jax.Sh...  79.4 us
    unnamed x1, local copies, waits for them, and re-layouts  1.92 us

profile of v2, /device:TPU:0, one launch (start us, length us, event | category | flops | bytes accessed | tf_op | source)
XLA Modules:
  0.0 81.4 jit_solution(9037512704357257701)
XLA Ops:
  0.0 79.4 %shard_map.46 = f32[64,2304]{1,0:T(8,128)} custom-call(s32[512]{0:T(512)} %order_in.1, bf16[512,9216]{1,0:T(8,128)(2,1)} %bitcast.4, bf16[512,512]{1,0:T(8,128)(2,1)} %bitcast.6, f32[18,18,128]{2,1,0:T(8,128)} %bitcast.7), custom_call_target="tpu_custom_call" | custom-call | tf_op jit(solution)/shard_map/pallas_call | solution.py:496
  79.5 1.9 %copy.6 = f32[2304,64]{0,1:T(8,128)} copy(f32[2304,64]{0,1:T(8,128)} %bitcast.5) | data formatting | bytes 1179648

commit v3 on v2

--- a/solution.py
+++ b/solution.py
@@ -27,11 +27,11 @@
 )
 SPLIT = (0, 1, 2)
 ORDER = (
-    -1, -1, -1, -1, 1, 2, 7, 130, 129, 17, 18, 23, -1, 4, -1, 10, 0, 20, 114, 26, 11, 128, 16, 27, 113, 39, 15, 31,
-    112, 3, -2, 32, 19, 14, 33, 42, 6, 36, 55, 30, 22, 13, 29, 12, 35, 28, 52, 48, 38, 51, 47, 34, 43, 68, 49, 5,
-    21, 54, 58, 44, 9, 37, 25, 45, 8, 24, 63, 74, 46, 84, 50, 53, 66, 60, 71, 64, 79, 59, 65, 75, 41, 95, 40, 67,
-    61, 70, 62, 77, 76, 81, 57, 69, 78, 87, 90, 56, 100, 93, 82, 106, 83, 73, 97, 80, 85, 86, 103, 94, 72, 96, 89,
-    92, 111, 110, 105, 99, 98, 101, 102, 91, 88, 107, 108, 109, 104,
+    -1, -1, -1, -1, 1, 2, 0, -1, 129, 17, 3, 128, 130, 18, 16, -1, 19, 15, 114, 112, 8, 31, 12, 24, 14, 28, 7, 30,
+    23, 34, -2, 11, 32, 27, 47, 35, 6, 22, 4, 40, 48, 20, 50, 10, 39, 26, 113, 13, 44, 51, 29, 33, 5, 66, 21, 63, 9,
+    56, 38, 25, 55, 42, 37, 54, 36, 72, 53, 49, 46, 43, 65, 60, 45, 76, 52, 71, 59, 79, 68, 41, 82, 67, 75, 61, 64,
+    84, 77, 58, 88, 70, 81, 74, 57, 62, 69, 83, 100, 87, 95, 93, 73, 98, 80, 97, 92, 85, 86, 91, 109, 96, 78, 103,
+    107, 90, 89, 99, 101, 94, 111, 108, 106, 102, 105, 110, 104,
 )
 
 

time: 81.5 us -> 81.3 us (level)
  no operation moved by 1% of the time
where the time goes in v3:
time: 81.3 us; the launch traced here: 81.2 us
  Pallas kernels  79.2 us (97%)
  local copies, waits for them, and re-layouts  1.92 us (2%)
    pallas_call x1, Pallas kernels, routed(): pl.pallas_call(functools.partial(kernel, size, nh, apo), out_shape=jax.Sh...  79.2 us
    unnamed x1, local copies, waits for them, and re-layouts  1.92 us

profile of v3, /device:TPU:0, one launch (start us, length us, event | category | flops | bytes accessed | tf_op | source)
XLA Modules:
  0.0 81.2 jit_solution(2612478751352200332)
XLA Ops:
  0.0 79.2 %shard_map.46 = f32[64,2304]{1,0:T(8,128)} custom-call(s32[512]{0:T(512)} %order_in.1, bf16[512,9216]{1,0:T(8,128)(2,1)} %bitcast.4, bf16[512,512]{1,0:T(8,128)(2,1)} %bitcast.6, f32[18,18,128]{2,1,0:T(8,128)} %bitcast.7), custom_call_target="tpu_custom_call" | custom-call | tf_op jit(solution)/shard_map/pallas_call | solution.py:496
  79.2 1.9 %copy.6 = f32[2304,64]{0,1:T(8,128)} copy(f32[2304,64]{0,1:T(8,128)} %bitcast.5) | data formatting | bytes 1179648
